TPU v7x, 32 devices: a whole 2x2x4 slice. The times are simulated.
32 devices in a mesh: dp: 4 (over x, core), tensor: 8 (over z, y).
Axes of the slice: x: 2, y: 2, z: 4, core: 2. Of those that a mesh axis runs over, the one named last changes fastest.
Arguments:
- activations: bfloat16 [2048, 28672], P('dp', 'tensor'), parts along dimension 0, may hold values from -6 to 6
- down_weight: bfloat16 [28672, 6144], P('tensor'), may hold values from -0.046875 to 0.046875
Outputs:
- projected: bfloat16 [2048, 6144], P(('dp', 'tensor')), parts along dimension 0
There are 4 independent parts, one for each index of `dp`. A program takes and returns all parts, laid end to end along the dimension named above; an argument that names none is the same for every part. Nothing has to cross between parts.
All inputs are finite; a program needn't handle non-finite values.
Results may differ from a plain program's by a relative error of at most 0.015.
Values may be sent and summed in bfloat16 or wider, within the bound.
A program may use at most 128 MiB of HBM per device.

v0:
```python
import functools
import math

import jax
import jax.numpy as jnp
import numpy as np
from jax import lax
from jax.experimental import pallas as pl
from jax.experimental.pallas import tpu as pltpu
from jax.sharding import PartitionSpec as P

INNER = 32
WEIGHT_SLOTS = 8
SECTIONS = 6
AHEAD = 2


def paley_matrix():
    modulus = 13
    residues = set((value * value % modulus for value in range(1, modulus)))
    jacobsthal = np.array(
        [
            [
                (
                    0.0
                    if row_at == col_at
                    else 1.0 if (col_at - row_at) % modulus in residues else -1.0
                )
                for col_at in range(modulus)
            ]
            for row_at in range(modulus)
        ]
    )
    confer = np.zeros((14, 14))
    confer[0, 1:] = 1.0
    confer[1:, 0] = 1.0
    confer[1:, 1:] = jacobsthal
    return np.kron(confer, np.array([[1.0, 1.0], [1.0, -1.0]])) + np.kron(
        np.eye(14), np.array([[1.0, -1.0], [-1.0, -1.0]])
    )


def sylvester(order):
    matrix = np.ones((1, 1))
    while matrix.shape[0] < order:
        matrix = np.kron(matrix, np.array([[1.0, 1.0], [1.0, -1.0]]))
    return matrix


def sine_terms():
    series = np.polynomial.chebyshev.Chebyshev.interpolate(
        lambda square: np.sinc(2.0 * np.sqrt(np.maximum(square, 0.0))), 8, domain=[0.0, 0.25]
    )
    power = series.convert(kind=np.polynomial.Polynomial, domain=[-1, 1], window=[-1, 1])
    return [float(value) for value in power.coef]


def butterfly(values):
    step = 1
    while step < len(values):
        result = list(values)
        for at in range(len(values)):
            if not at & step:
                result[at] = values[at] + values[at + step]
                result[at + step] = values[at] - values[at + step]
        values, step = result, step * 2
    return values


def flipped(position, mask):
    result, bit = position, 1
    while bit <= mask:
        if mask & bit:
            result = result + (1 - 2 * ((position // bit) % 2)) * bit
        bit *= 2
    return result


def mirrored(position, groups):
    result, bit = 0, 1
    while bit < groups:
        result = result + ((position // bit) % 2) * (groups // 2 // bit)
        bit *= 2
    return result


def kernel(
    groups, chunks, tile, normal_scale, terms,
    act_ref, weight_ref, table_ref, out_ref,
    x_buf, rot, q_buf, d_buf, part, w_buf, *rest,
):
    stages = groups.bit_length() - 1
    recv_bufs = rest[:stages]
    (x_send, x_recv, own_sem, q_send, q_recv, r_send, r_recv, w_sem) = rest[stages:]
    me = lax.axis_index("tensor")
    rows = x_buf.shape[2]
    width = x_buf.shape[3]
    inner = table_ref.shape[0]
    subs = width // inner
    tiles = weight_ref.shape[1] // tile
    section_tiles = tiles // SECTIONS
    section_width = section_tiles * tile
    place = mirrored(me, groups)
    peers = [(mask, flipped(me, mask)) for mask in range(groups - 1, 0, -1)]

    def weight_copy(step):
        column = pl.multiple_of((step % tiles) * tile, 128)
        slot = step % WEIGHT_SLOTS
        return pltpu.make_async_copy(
            weight_ref.at[:, pl.ds(column, tile)], w_buf.at[slot], w_sem.at[slot]
        )

    def own_rows(chunk):
        first = pl.multiple_of(me * (chunks * rows) + chunk * rows, rows)
        return pltpu.make_async_copy(
            act_ref.at[pl.ds(first, rows), :], x_buf.at[chunk, me], own_sem.at[chunk]
        )

    def x_copy(chunk, mask, peer):
        first = pl.multiple_of(peer * (chunks * rows) + chunk * rows, rows)
        return pltpu.make_async_remote_copy(
            src_ref=act_ref.at[pl.ds(first, rows), :],
            dst_ref=x_buf.at[chunk, me],
            send_sem=x_send.at[chunk, mask],
            recv_sem=x_recv.at[chunk, mask],
            device_id={"tensor": peer},
            device_id_type=pl.DeviceIdType.MESH,
        )

    def q_copy(chunk, mask, peer):
        return pltpu.make_async_remote_copy(
            src_ref=q_buf.at[chunk, peer],
            dst_ref=d_buf.at[chunk, place],
            send_sem=q_send.at[chunk, mask],
            recv_sem=q_recv.at[chunk, mask],
            device_id={"tensor": peer},
            device_id_type=pl.DeviceIdType.MESH,
        )

    def half_at(stage):
        start, span, kept = 0, groups, 0
        for at in range(stage + 1):
            span //= 2
            start = kept
            bit = (me // (1 << at)) % 2
            kept = start + bit * span
            sent = start + (1 - bit) * span
        return kept, sent, span

    def r_copy(chunk, stage, section):
        kept, sent, span = half_at(stage)
        column = pl.ds(section * section_width, section_width)
        return pltpu.make_async_remote_copy(
            src_ref=part.at[chunk, pl.ds(sent, span), :, column],
            dst_ref=recv_bufs[stage].at[chunk, :, :, column],
            send_sem=r_send.at[chunk, stage, section],
            recv_sem=r_recv.at[chunk, stage, section],
            device_id={"tensor": flipped(me, 1 << stage)},
            device_id_type=pl.DeviceIdType.MESH,
        )

    barrier = pltpu.get_barrier_semaphore()
    for mask, peer in peers:
        pl.semaphore_signal(
            barrier, inc=1, device_id={"tensor": peer}, device_id_type=pl.DeviceIdType.MESH
        )
    pl.semaphore_wait(barrier, groups - 1)

    def exchange(chunk):
        for mask, peer in peers:
            x_copy(chunk, mask, peer).start()
        own_rows(chunk).start()

    for chunk in range(min(AHEAD, chunks)):
        exchange(chunk)
    for step in range(WEIGHT_SLOTS):
        weight_copy(step).start()

    def rotate(chunk):
        for sub in range(subs):
            block = x_buf[chunk, :, :, sub * inner:(sub + 1) * inner]
            rot[sub] = jnp.dot(
                block.reshape(groups * rows, inner), table_ref[...],
                preferred_element_type=jnp.float32,
            ).reshape(groups, rows, inner)

        def mix(at, tops):
            column = pl.ds(pl.multiple_of(at * 128, 128), 128)
            result = []
            for index in range(rows // 8):
                line = pl.ds(index * 8, 8)
                values = butterfly(
                    [rot[sub, group, line, column] for group in range(groups) for sub in range(subs)]
                )
                top = tops[index]
                for block_at, value in enumerate(values):
                    rot[block_at % subs, block_at // subs, line, column] = value
                    top = jnp.maximum(top, jnp.abs(value))
                result.append(top)
            return tuple(result)

        tops = lax.fori_loop(
            0, inner // 128, mix,
            tuple(jnp.zeros((8, 128), jnp.float32) for _ in range(rows // 8)),
        )
        largest = jnp.concatenate([jnp.max(top, axis=1, keepdims=True) for top in tops], axis=0)
        token_scale = jnp.maximum(largest * normal_scale, 1.0)
        into = 7.0 * normal_scale / token_scale
        back = token_scale / 7.0

        @pl.loop(0, groups)
        def _(group):
            for sub in range(subs):
                levels = rot[sub, group] * into
                offset = levels - jnp.floor(levels + 0.5)
                square = offset * offset
                series = jnp.full_like(square, terms[-1])
                for term in terms[-2::-1]:
                    series = series * square + term
                q_buf[chunk, group, :, sub * inner:(sub + 1) * inner] = (
                    (levels - offset * series) * back
                ).astype(jnp.bfloat16)

    def finish_tokens(chunk):
        own_rows(chunk).wait()
        for mask, peer in peers:
            x_copy(chunk, mask, peer).wait_recv()
        rotate(chunk)
        for mask, peer in peers:
            q_copy(chunk, mask, peer).start()
        d_buf[chunk, place] = q_buf[chunk, me]
        if chunk + AHEAD < chunks:
            exchange(chunk + AHEAD)

    def reduce_stage(chunk, stage, section):
        r_copy(chunk, stage, section).wait_recv()
        kept, sent, span = half_at(stage)
        last = stage == stages - 1
        piece = section_width // 2

        @pl.loop(0, span * 2)
        def _(at):
            block = at // 2
            column = pl.ds(pl.multiple_of(section * section_width + (at % 2) * piece, 128), piece)
            total = (
                part[chunk, kept + block, :, column].astype(jnp.float32)
                + recv_bufs[stage][chunk, block, :, column].astype(jnp.float32)
            ).astype(jnp.bfloat16)
            if last:
                out_ref[pl.ds(chunk * rows, rows), column] = total
            else:
                part[chunk, kept + block, :, column] = total

        if not last:
            r_copy(chunk, stage + 1, section).start()

    def project(chunk):
        for mask, peer in peers:
            q_copy(chunk, mask, peer).wait_recv()
        for section in range(SECTIONS):
            @pl.loop(section * section_tiles, (section + 1) * section_tiles)
            def _(at):
                step = chunk * tiles + at
                weight_copy(step).wait()
                part[chunk, :, :, pl.ds(pl.multiple_of(at * tile, 128), tile)] = (
                    jnp.dot(
                        d_buf[chunk].reshape(groups * rows, width),
                        w_buf[step % WEIGHT_SLOTS],
                        preferred_element_type=jnp.float32,
                    )
                    .astype(jnp.bfloat16)
                    .reshape(groups, rows, tile)
                )

                @pl.when(step + WEIGHT_SLOTS < chunks * tiles)
                def _():
                    weight_copy(step + WEIGHT_SLOTS).start()

            r_copy(chunk, 0, section).start()

    for chunk in range(min(AHEAD, chunks)):
        finish_tokens(chunk)
    for turn in range(chunks + stages):
        if turn < chunks:
            project(turn)
        for stage in range(stages):
            chunk = turn - 1 - stage
            if 0 <= chunk < chunks:
                for section in range(SECTIONS):
                    reduce_stage(chunk, stage, section)
        if AHEAD <= turn + AHEAD < chunks:
            finish_tokens(turn + AHEAD)

    for chunk in range(chunks):
        for mask, peer in peers:
            x_copy(chunk, mask, peer).wait_send()
            q_copy(chunk, mask, peer).wait_send()
        for stage in range(stages):
            for section in range(SECTIONS):
                r_copy(chunk, stage, section).wait_send()


def shards(activations, down_weight):
    count_rows, width = activations.shape
    features = down_weight.shape[1]
    groups = lax.axis_size("tensor")
    stages = groups.bit_length() - 1
    own = count_rows // groups
    rows = 16
    chunks = own // rows
    tile = 512
    table = jnp.asarray(np.kron(sylvester(INNER), paley_matrix()), jnp.bfloat16)
    inner = table.shape[0]
    bf16, dma = jnp.bfloat16, pltpu.SemaphoreType.DMA
    body = functools.partial(
        kernel, groups, chunks, tile, 1.0 / math.sqrt(width * groups), sine_terms()
    )
    return pl.pallas_call(
        body,
        out_shape=jax.ShapeDtypeStruct((own, features), bf16),
        in_specs=[
            pl.BlockSpec(memory_space=pl.ANY),
            pl.BlockSpec(memory_space=pl.ANY),
            pl.BlockSpec(memory_space=pltpu.VMEM),
        ],
        out_specs=pl.BlockSpec(memory_space=pltpu.VMEM),
        scratch_shapes=[
            pltpu.VMEM((chunks, groups, rows, width), bf16),
            pltpu.VMEM((width // inner, groups, rows, inner), jnp.float32),
            pltpu.VMEM((chunks, groups, rows, width), bf16),
            pltpu.VMEM((chunks, groups, rows, width), bf16),
            pltpu.VMEM((chunks, groups, rows, features), bf16),
            pltpu.VMEM((WEIGHT_SLOTS, width, tile), bf16),
        ]
        + [
            pltpu.VMEM((chunks, groups >> (stage + 1), rows, features), bf16)
            for stage in range(stages)
        ]
        + [
            dma((chunks, groups)),
            dma((chunks, groups)),
            dma((chunks,)),
            dma((chunks, groups)),
            dma((chunks, groups)),
            dma((chunks, stages, SECTIONS)),
            dma((chunks, stages, SECTIONS)),
            dma((WEIGHT_SLOTS,)),
        ],
        compiler_params=pltpu.CompilerParams(
            collective_id=0, has_side_effects=True, vmem_limit_bytes=60 * 1024 * 1024
        ),
        name="rotate_quantize_project",
    )(activations, down_weight, table)


def solution(mesh):
    placed = (P("dp", "tensor"), P("tensor", None))
    return jax.shard_map(
        shards, mesh=mesh, in_specs=placed, out_specs=P(("dp", "tensor"), None), check_vma=False
    )
```

profile of v0, /device:TPU:0, one launch (start us, length us, event | category | flops | bytes accessed | tf_op | source)
XLA Modules:
  0.0 212.4 jit_solution(14519173111976821401)
XLA Ops:
  0.0 210.4 %rotate_quantize_project.1 = bf16[64,6144]{1,0:T(8,128)(2,1)} custom-call(bf16[512,3584]{1,0:T(8,128)(2,1)} %act_ref.1, bf16[3584,6144]{1,0:T(8,128)(2,1)} %weight_ref.1, bf16[896,896]{1,0:T(8,128)(2,1)} %constant.2.clone.table_ref), custom_call_target="tpu_custom_call" | custom-call | tf_op jit(solution)/shard_map/rotate_quantize_project/pallas_call | solution.py:318
  210.4 2.1 copy.5
where the time goes:
time: 213 us; the launch traced here: 212 us
  Pallas kernels  210 us (99%)
    pallas_call x1, Pallas kernels, shards(): pl.pallas_call(body, out_shape=jax.ShapeDtypeStruct((own, features), bf16...  210 us

commit v1 on v0

v1 whole, which is shorter than its diff:
```python
import functools
import math

import jax
import jax.numpy as jnp
import numpy as np
from jax import lax
from jax.experimental import pallas as pl
from jax.experimental.pallas import tpu as pltpu
from jax.sharding import PartitionSpec as P

INNER = 32
RESIDENT = 7
STREAM = 2
SECTIONS = 6
AHEAD = 2
BEHIND = 1
HOLD = 3


def paley_matrix():
    modulus = 13
    residues = set((value * value % modulus for value in range(1, modulus)))
    jacobsthal = np.array(
        [
            [
                (
                    0.0
                    if row_at == col_at
                    else 1.0 if (col_at - row_at) % modulus in residues else -1.0
                )
                for col_at in range(modulus)
            ]
            for row_at in range(modulus)
        ]
    )
    confer = np.zeros((14, 14))
    confer[0, 1:] = 1.0
    confer[1:, 0] = 1.0
    confer[1:, 1:] = jacobsthal
    return np.kron(confer, np.array([[1.0, 1.0], [1.0, -1.0]])) + np.kron(
        np.eye(14), np.array([[1.0, -1.0], [-1.0, -1.0]])
    )


def sylvester(order):
    matrix = np.ones((1, 1))
    while matrix.shape[0] < order:
        matrix = np.kron(matrix, np.array([[1.0, 1.0], [1.0, -1.0]]))
    return matrix


def sine_terms():
    series = np.polynomial.chebyshev.Chebyshev.interpolate(
        lambda square: np.sinc(2.0 * np.sqrt(np.maximum(square, 0.0))), 8, domain=[0.0, 0.25]
    )
    power = series.convert(kind=np.polynomial.Polynomial, domain=[-1, 1], window=[-1, 1])
    return [float(value) for value in power.coef]


def butterfly(values):
    step = 1
    while step < len(values):
        result = list(values)
        for at in range(len(values)):
            if not at & step:
                result[at] = values[at] + values[at + step]
                result[at + step] = values[at] - values[at + step]
        values, step = result, step * 2
    return values


def flipped(position, mask):
    result, bit = position, 1
    while bit <= mask:
        if mask & bit:
            result = result + (1 - 2 * ((position // bit) % 2)) * bit
        bit *= 2
    return result


def mirrored(position, groups):
    result, bit = 0, 1
    while bit < groups:
        result = result + ((position // bit) % 2) * (groups // 2 // bit)
        bit *= 2
    return result


def kernel(
    groups, chunks, tile, normal_scale, terms,
    act_ref, weight_ref, table_hbm, out_ref,
    table_ref, x_buf, rot, d_buf, flat, part, w_buf, *rest,
):
    stages = groups.bit_length() - 1
    recv_bufs = rest[:stages]
    (sent_sem, x_recv, q_recv, r_send, r_recv, last_recv, w_sem, t_sem) = rest[stages:]
    me = lax.axis_index("tensor")
    rows = x_buf.shape[2]
    width = x_buf.shape[3]
    inner = table_ref.shape[0]
    subs = width // inner
    features = weight_ref.shape[1]
    tiles = features // tile
    section_tiles = tiles // SECTIONS
    section_width = section_tiles * tile
    final = chunks - 1
    slots = part.shape[0]
    lags = [*range(1, stages - 1), stages, stages + 2]
    place = mirrored(me, groups)
    peers = [(mask, flipped(me, mask)) for mask in range(1, groups)]

    streamed = tiles - RESIDENT

    def weight_copy(at, slot):
        column = pl.multiple_of(at * tile, 128)
        return pltpu.make_async_copy(
            weight_ref.at[:, pl.ds(column, tile)], w_buf.at[slot], w_sem.at[slot]
        )

    def stream_copy(step):
        return weight_copy(RESIDENT + step % streamed, RESIDENT + step % STREAM)

    def own_rows(chunk):
        first = pl.multiple_of(me * (chunks * rows) + chunk * rows, rows)
        return pltpu.make_async_copy(
            act_ref.at[pl.ds(first, rows), :], x_buf.at[chunk, me], x_recv.at[chunk]
        )

    def x_copy(chunk, peer):
        first = pl.multiple_of(peer * (chunks * rows) + chunk * rows, rows)
        return pltpu.make_async_remote_copy(
            src_ref=act_ref.at[pl.ds(first, rows), :],
            dst_ref=x_buf.at[chunk, me],
            send_sem=sent_sem.at[chunk],
            recv_sem=x_recv.at[chunk],
            device_id={"tensor": peer},
            device_id_type=pl.DeviceIdType.MESH,
        )

    def q_copy(chunk, peer):
        return pltpu.make_async_remote_copy(
            src_ref=x_buf.at[chunk, peer],
            dst_ref=d_buf.at[chunk, place],
            send_sem=sent_sem.at[chunk],
            recv_sem=q_recv.at[chunk],
            device_id={"tensor": peer},
            device_id_type=pl.DeviceIdType.MESH,
        )

    def whole(ref, sem):
        return pltpu.make_async_copy(ref, ref, sem)

    def half_at(stage):
        start, span, kept = 0, groups, 0
        for at in range(stage + 1):
            span //= 2
            start = kept
            bit = (me // (1 << at)) % 2
            kept = start + bit * span
            sent = start + (1 - bit) * span
        return kept, sent, span

    def r_copy(chunk, stage, section=None, sem=None):
        kept, sent, span = half_at(stage)
        first, extent = 0, features
        if section is not None:
            first, extent = pl.multiple_of(section * section_width, 128), section_width
        column = pl.ds(first, extent)
        return pltpu.make_async_remote_copy(
            src_ref=part.at[chunk % slots, pl.ds(sent, span), :, column],
            dst_ref=recv_bufs[stage].at[chunk, :, :, column],
            send_sem=r_send.at[chunk],
            recv_sem=r_recv.at[chunk, stage] if sem is None else sem,
            device_id={"tensor": flipped(me, 1 << stage)},
            device_id_type=pl.DeviceIdType.MESH,
        )

    barrier = pltpu.get_barrier_semaphore()
    for mask, peer in peers:
        pl.semaphore_signal(
            barrier, inc=1, device_id={"tensor": peer}, device_id_type=pl.DeviceIdType.MESH
        )
    pl.semaphore_wait(barrier, groups - 1)

    def exchange(chunk):
        for mask, peer in peers:
            x_copy(chunk, peer).start()
        own_rows(chunk).start()

    for chunk in range(min(AHEAD, chunks)):
        exchange(chunk)
    table_copy = pltpu.make_async_copy(table_hbm, table_ref, t_sem)
    table_copy.start()
    table_copy.wait()
    for at in range(RESIDENT):
        weight_copy(at, at).start()
    for step in range(STREAM):
        stream_copy(step).start()

    def rotate(chunk):
        for sub in range(subs):
            block = x_buf[chunk, :, :, sub * inner:(sub + 1) * inner]
            rot[sub] = jnp.dot(
                block.reshape(groups * rows, inner), table_ref[...],
                preferred_element_type=jnp.float32,
            ).reshape(groups, rows, inner)

        def mix(at, tops):
            column = pl.ds(pl.multiple_of(at * 128, 128), 128)
            result = []
            for index in range(rows // 8):
                line = pl.ds(index * 8, 8)
                values = butterfly(
                    [rot[sub, group, line, column] for group in range(groups) for sub in range(subs)]
                )
                top = tops[index]
                for block_at, value in enumerate(values):
                    rot[block_at % subs, block_at // subs, line, column] = value
                    top = jnp.maximum(top, jnp.abs(value))
                result.append(top)
            return tuple(result)

        tops = lax.fori_loop(
            0, inner // 128, mix,
            tuple(jnp.zeros((8, 128), jnp.float32) for _ in range(rows // 8)),
        )
        largest = jnp.concatenate([jnp.max(top, axis=1, keepdims=True) for top in tops], axis=0)
        token_scale = jnp.maximum(largest * normal_scale, 1.0)
        into = 7.0 * normal_scale / token_scale
        back = token_scale / 7.0

        @pl.loop(0, groups)
        def _(group):
            for sub in range(subs):
                levels = rot[sub, group] * into
                offset = levels - jnp.floor(levels + 0.5)
                square = offset * offset
                series = jnp.full_like(square, terms[-1])
                for term in terms[-2::-1]:
                    series = series * square + term
                x_buf[chunk, group, :, sub * inner:(sub + 1) * inner] = (
                    (levels - offset * series) * back
                ).astype(jnp.bfloat16)

    def finish_tokens(chunk):
        whole(x_buf.at[chunk], x_recv.at[chunk]).wait()
        rotate(chunk)
        d_buf[chunk, place] = x_buf[chunk, me]
        for mask, peer in peers:
            q_copy(chunk, peer).start()

        @pl.when(chunk + AHEAD < chunks)
        def _():
            exchange(chunk + AHEAD)

    def add_up(chunk, stage, first, extent):
        kept, sent, span = half_at(stage)
        pieces = extent // section_width

        @pl.loop(0, span * pieces)
        def _(at):
            block = at // pieces
            column = pl.ds(pl.multiple_of(first + (at % pieces) * section_width, 128), section_width)
            total = (
                part[chunk % slots, kept + block, :, column].astype(jnp.float32)
                + recv_bufs[stage][chunk, block, :, column].astype(jnp.float32)
            ).astype(jnp.bfloat16)
            if stage == stages - 1:
                out_ref[pl.ds(pl.multiple_of(chunk * rows, rows), rows), column] = total
            else:
                part[chunk % slots, kept + block, :, column] = total

    def reduce_chunk(chunk, stage):
        whole(recv_bufs[stage].at[chunk], r_recv.at[chunk, stage]).wait()
        add_up(chunk, stage, 0, features)
        if stage < stages - 1:
            r_copy(chunk, stage + 1).start()

    def reduce_last(stage, section):
        r_copy(final, stage, section, last_recv.at[stage, section]).wait_recv()
        add_up(final, stage, section * section_width, section_width)
        if stage < stages - 1:
            r_copy(final, stage + 1, section, last_recv.at[stage + 1, section]).start()

    def product(chunk, at, slot):
        part[chunk % slots, :, :, pl.ds(pl.multiple_of(at * tile, 128), tile)] = (
            jnp.dot(
                flat[...],
                w_buf[slot],
                preferred_element_type=jnp.float32,
            )
            .astype(jnp.bfloat16)
            .reshape(groups, rows, tile)
        )

    def multiply(chunk, section):
        @pl.loop(section * section_tiles, (section + 1) * section_tiles)
        def _(at):
            step = chunk * streamed + at - RESIDENT

            @pl.when((chunk == 0) & (at < RESIDENT))
            def _():
                weight_copy(at, at).wait()

            if streamed:
                @pl.when(at >= RESIDENT)
                def _():
                    stream_copy(step).wait()

                resident = at // RESIDENT
                product(chunk, at, (1 - resident) * at + resident * (RESIDENT + step % STREAM))

                @pl.when((at >= RESIDENT) & (step + STREAM < chunks * streamed))
                def _():
                    stream_copy(step + STREAM).start()
            else:
                product(chunk, at, at)

    def sends_done(chunk):
        whole(part.at[chunk % slots, pl.ds(0, groups - 1)], r_send.at[chunk]).wait()

    def gather(chunk):
        others = pl.ds(0, groups - 1)
        whole(d_buf.at[chunk, others], q_recv.at[chunk]).wait()
        flat[...] = d_buf[chunk].reshape(groups * rows, width)

    @pl.loop(0, final + BEHIND)
    def _(turn):
        @pl.when(turn < chunks)
        def _():
            finish_tokens(turn)

        @pl.when(turn >= BEHIND)
        def _():
            chunk = turn - BEHIND
            gather(chunk)

            @pl.when(chunk >= slots)
            def _():
                sends_done(chunk - slots)

            for stage in range(stages):
                @pl.when(chunk >= lags[stage])
                def _():
                    reduce_chunk(chunk - lags[stage], stage)

            @pl.loop(0, SECTIONS)
            def _(section):
                multiply(chunk, section)
                r_copy(chunk, 0, section).start()

    def reduce_back(most, least, stage):
        for back in range(min(most, final), least - 1, -1):
            reduce_chunk(final - back, stage)

    gather(final)
    if final >= slots:
        sends_done(final - slots)
        reduce_chunk(final - slots, stages - 1)
    for stage in range(stages - 2, 0, -1):
        reduce_back(lags[stage], stage + 1, stage)

    @pl.loop(0, SECTIONS)
    def _(section):
        multiply(final, section)
        r_copy(final, 0, section, last_recv.at[0, section]).start()

        @pl.when(section == HOLD - 1)
        def _():
            reduce_back(1, 1, 0)

        @pl.when(section >= HOLD)
        def _():
            reduce_last(0, section - HOLD)

    reduce_last(0, SECTIONS - HOLD)
    for stage in range(1, stages - 1):
        reduce_back(stage, 1, stage)
        for section in range(SECTIONS):
            if stage == 1 and section + 1 < HOLD:
                reduce_last(0, SECTIONS - HOLD + 1 + section)
            reduce_last(stage, section)
    reduce_back(slots - 1, 1, stages - 1)

    @pl.loop(0, SECTIONS)
    def _(section):
        reduce_last(stages - 1, section)

    @pl.loop(0, chunks)
    def _(chunk):
        whole(x_buf.at[pl.ds(0, 2), pl.ds(0, groups - 1)], sent_sem.at[chunk]).wait()

    @pl.loop(chunks - slots, chunks)
    def _(chunk):
        sends_done(chunk)


def shards(activations, down_weight):
    count_rows, width = activations.shape
    features = down_weight.shape[1]
    groups = lax.axis_size("tensor")
    stages = groups.bit_length() - 1
    own = count_rows // groups
    rows = 8
    chunks = own // rows
    tile = 512
    table = jnp.asarray(np.kron(sylvester(INNER), paley_matrix()), jnp.bfloat16)
    inner = table.shape[0]
    bf16, dma = jnp.bfloat16, pltpu.SemaphoreType.DMA
    body = functools.partial(
        kernel, groups, chunks, tile, 1.0 / math.sqrt(width * groups), sine_terms()
    )
    return pl.pallas_call(
        body,
        out_shape=jax.ShapeDtypeStruct((own, features), bf16),
        in_specs=[
            pl.BlockSpec(memory_space=pltpu.HBM),
            pl.BlockSpec(memory_space=pltpu.HBM),
            pl.BlockSpec(memory_space=pltpu.HBM),
        ],
        out_specs=pl.BlockSpec(memory_space=pltpu.VMEM),
        scratch_shapes=[
            pltpu.VMEM((inner, inner), bf16),
            pltpu.VMEM((chunks, groups, rows, width), bf16),
            pltpu.VMEM((width // inner, groups, rows, inner), jnp.float32),
            pltpu.VMEM((chunks, groups, rows, width), bf16),
            pltpu.VMEM((groups * rows, width), bf16),
            pltpu.VMEM((min(stages + 2, chunks), groups, rows, features), bf16),
            pltpu.VMEM((RESIDENT + STREAM, width, tile), bf16),
        ]
        + [
            pltpu.VMEM((chunks, groups >> (stage + 1), rows, features), bf16)
            for stage in range(stages)
        ]
        + [
            dma((chunks,)),
            dma((chunks,)),
            dma((chunks,)),
            dma((chunks,)),
            dma((chunks, stages)),
            dma((stages, SECTIONS)),
            dma((RESIDENT + STREAM,)),
            dma,
        ],
        compiler_params=pltpu.CompilerParams(
            collective_id=0, has_side_effects=True, vmem_limit_bytes=53 * 1024 * 1024
        ),
        name="rotate_quantize_project",
    )(activations, down_weight, table)


def solution(mesh):
    placed = (P("dp", "tensor"), P("tensor", None))
    return jax.shard_map(
        shards, mesh=mesh, in_specs=placed, out_specs=P(("dp", "tensor"), None), check_vma=False
    )
```

time: 213 us -> 208 us (0.977)
  Pallas kernels: 210 us -> 206 us
    pallas_call x1, Pallas kernels: 210 us -> 206 us  [shards(): pl.pallas_call(body, out_shape=jax.ShapeDtypeStruct((own, features), bf16...]
where the time goes in v1:
time: 208 us; the launch traced here: 207 us
  Pallas kernels  206 us (99%)
    pallas_call x1, Pallas kernels, shards(): pl.pallas_call(body, out_shape=jax.ShapeDtypeStruct((own, features), bf16...  206 us

profile of v1, /device:TPU:0, one launch (start us, length us, event | category | flops | bytes accessed | tf_op | source)
XLA Modules:
  0.0 207.1 jit_solution(4681478755566694267)
XLA Ops:
  0.0 206.3 %rotate_quantize_project.1 = bf16[64,6144]{1,0:T(8,128)(2,1)S(1)} custom-call(bf16[512,3584]{1,0:T(8,128)(2,1)} %act_ref.1, bf16[3584,6144]{1,0:T(8,128)(2,1)} %weight_ref.1, bf16[896,896]{1,0:T(8,128)(2,1)} %constant.2.clone.table_hbm), custom_call_target="tpu_custom_call" | custom-call | tf_op jit(solution)/shard_map/rotate_quantize_project/pallas_call | solution.py:414
  206.3 0.9 copy.5

commit v2 on v1

--- a/solution.py
+++ b/solution.py
@@ -119,7 +119,7 @@
         )
 
     def stream_copy(step):
-        return weight_copy(RESIDENT + step % streamed, RESIDENT + step % STREAM)
+        return weight_copy(2 * (step % streamed) + 1, RESIDENT + step % STREAM)
 
     def own_rows(chunk):
         first = pl.multiple_of(me * (chunks * rows) + chunk * rows, rows)
@@ -193,10 +193,11 @@
     table_copy = pltpu.make_async_copy(table_hbm, table_ref, t_sem)
     table_copy.start()
     table_copy.wait()
-    for at in range(RESIDENT):
-        weight_copy(at, at).start()
-    for step in range(STREAM):
-        stream_copy(step).start()
+    for at in range(tiles):
+        if at % 2 == 0 or at > 2 * streamed:
+            weight_copy(at, at - min(at // 2, streamed)).start()
+        elif at // 2 < STREAM:
+            stream_copy(at // 2).start()
 
     def rotate(chunk):
         for sub in range(subs):
@@ -297,25 +298,25 @@
     def multiply(chunk, section):
         @pl.loop(section * section_tiles, (section + 1) * section_tiles)
         def _(at):
-            step = chunk * streamed + at - RESIDENT
-
-            @pl.when((chunk == 0) & (at < RESIDENT))
+            pair, odd = at // 2, at % 2
+            paired = 1 - at // (2 * streamed)
+            passing = odd * paired
+            step = chunk * streamed + pair
+            kept = paired * pair + (1 - paired) * (at - streamed)
+
+            @pl.when((chunk == 0) & (passing == 0))
             def _():
-                weight_copy(at, at).wait()
-
-            if streamed:
-                @pl.when(at >= RESIDENT)
-                def _():
-                    stream_copy(step).wait()
-
-                resident = at // RESIDENT
-                product(chunk, at, (1 - resident) * at + resident * (RESIDENT + step % STREAM))
-
-                @pl.when((at >= RESIDENT) & (step + STREAM < chunks * streamed))
-                def _():
-                    stream_copy(step + STREAM).start()
-            else:
-                product(chunk, at, at)
+                weight_copy(at, kept).wait()
+
+            @pl.when(passing == 1)
+            def _():
+                stream_copy(step).wait()
+
+            product(chunk, at, (1 - passing) * kept + passing * (RESIDENT + step % STREAM))
+
+            @pl.when((passing == 1) & (step + STREAM < chunks * streamed))
+            def _():
+                stream_copy(step + STREAM).start()
 
     def sends_done(chunk):
         whole(part.at[chunk % slots, pl.ds(0, groups - 1)], r_send.at[chunk]).wait()
@@ -366,7 +367,7 @@
         multiply(final, section)
         r_copy(final, 0, section, last_recv.at[0, section]).start()
 
-        @pl.when(section == HOLD - 1)
+        @pl.when(section == 1)
         def _():
             reduce_back(1, 1, 0)
 

time: 208 us -> 207 us (level)
  no operation moved by 1% of the time
where the time goes in v2:
time: 207 us
  Pallas kernels  206 us (100%)
    pallas_call x1, Pallas kernels, shards(): pl.pallas_call(body, out_shape=jax.ShapeDtypeStruct((own, features), bf16...  206 us

profile of v2, /device:TPU:0, one launch (start us, length us, event | category | flops | bytes accessed | tf_op | source)
XLA Modules:
  0.0 206.8 jit_solution(3112171428270432139)
XLA Ops:
  0.0 205.9 %rotate_quantize_project.1 = bf16[64,6144]{1,0:T(8,128)(2,1)S(1)} custom-call(bf16[512,3584]{1,0:T(8,128)(2,1)} %act_ref.1, bf16[3584,6144]{1,0:T(8,128)(2,1)} %weight_ref.1, bf16[896,896]{1,0:T(8,128)(2,1)} %constant.2.clone.table_hbm), custom_call_target="tpu_custom_call" | custom-call | tf_op jit(solution)/shard_map/rotate_quantize_project/pallas_call | solution.py:415
  205.9 0.9 copy.5
